TPU v7x, 32 devices: a whole 2x2x4 slice. The times are simulated.
32 devices in a mesh: ka: 8 (over z, x), row: 4 (over y, core).
Axes of the slice: x: 2, y: 2, z: 4, core: 2. Of those that a mesh axis runs over, the one named last changes fastest.
Arguments:
- gauge: bfloat16 [32, 2, 384, 384], P(('ka', 'row')), may hold values from -3 to 3
- energies: float32 [32, 384], P(('ka', 'row')), may hold values from -5 to 5
- kmesh: int32 [3, 32], replicated, may hold values from 0 to 11
- lattice: int32 [3, 256], P(None, 'row'), may hold values from -8 to 8
- degeneracy: int32 [256], P('row'), may hold values from 1 to 8
- path: int32 [3, 8], replicated, may hold values from 0 to 63
Outputs:
- lattice_h: bfloat16 [256, 384, 768], P('row', 'ka')
- path_h: float32 [8, 384, 768], P('row', 'ka')
All inputs are finite; a program needn't handle non-finite values.
Results may differ from a plain program's by a relative error of at most 0.006.
Values may be sent and summed in bfloat16 or wider, within the bound.
No kernel may reach another device: no remote copies, remote signals or barrier semaphores. Data moves between devices by JAX's collectives and lax.ppermute only.
A program may use at most 64 MiB of HBM per device.

v0:
```python
import math
import jax
import jax.numpy as jnp
from jax import lax
from jax.sharding import PartitionSpec as P

MESH = 12
PATH_DEN = 64


def phases(vectors, coords):
    windings = jnp.mod(jnp.sum(vectors[:, :, None] * coords[:, None, :], 0), MESH)
    angles = windings.astype(jnp.float32) * (2.0 * math.pi / MESH)
    return jnp.concatenate([jnp.cos(angles), jnp.sin(angles)], 0).astype(jnp.bfloat16)


def path_factors(path_coords, vectors, counts):
    windings = jnp.mod(jnp.sum(path_coords[:, :, None] * vectors[:, None, :], 0), PATH_DEN)
    angles = windings.astype(jnp.float32) * (2.0 * math.pi / PATH_DEN)
    weights = 1.0 / counts.astype(jnp.float32)
    return jnp.concatenate(
        [jnp.cos(angles) * weights[None, :], jnp.sin(angles) * weights[None, :]], 0
    ).astype(jnp.bfloat16)


def combine_fourier(products, scale_by):
    real_part = products[0, :, :, 0] + products[1, :, :, 1]
    imag_part = products[0, :, :, 1] - products[1, :, :, 0]
    return jnp.concatenate([real_part, imag_part], -1) / scale_by


def combine_path(products):
    real_part = products[0, :, :, 0] - products[1, :, :, 1]
    imag_part = products[0, :, :, 1] + products[1, :, :, 0]
    return jnp.concatenate([real_part, imag_part], -1)


def local(gauge, energies, kmesh, lattice, degeneracy, path):
    per_device = gauge.shape[0]
    orbitals = gauge.shape[2]
    ka_count = lax.axis_size("ka")
    row_count = lax.axis_size("row")
    k_total = kmesh.shape[1]
    path_dev = path.shape[1] // row_count
    scaled = (energies[:, None, :, None] * gauge.astype(jnp.float32)).astype(jnp.bfloat16)
    stacked = jnp.concatenate([gauge[:, 0], gauge[:, 1]], 1)
    partner = jnp.concatenate(
        [
            jnp.concatenate([scaled[:, 0], scaled[:, 1]], 2),
            jnp.concatenate([scaled[:, 1], -scaled[:, 0]], 2),
        ],
        1,
    )
    rotated = jnp.einsum(
        "kna,knb->kab", stacked, partner, preferred_element_type=jnp.float32
    ).astype(jnp.bfloat16)
    arrived = lax.all_to_all(rotated, "ka", split_axis=1, concat_axis=0, tiled=True)
    local_rows = arrived.shape[1]
    lattice_rows = lattice.shape[1]
    k_order = (
        kmesh.reshape(3, ka_count, row_count, per_device).transpose(0, 2, 1, 3).reshape(3, k_total)
    )
    vectors_all, counts_all = (
        lax.all_gather(lattice, "row", axis=1, tiled=True),
        lax.all_gather(degeneracy, "row", axis=0, tiled=True),
    )
    total_vectors = vectors_all.shape[1]
    own_path = lax.dynamic_slice_in_dim(path, lax.axis_index("row") * path_dev, path_dev, 1)
    factors_path = path_factors(own_path, vectors_all, counts_all).astype(jnp.float32)
    factors_mesh = phases(vectors_all, k_order).astype(jnp.float32)
    with_cos = jnp.dot(
        factors_path,
        factors_mesh[:total_vectors],
        preferred_element_type=jnp.float32,
        precision=lax.Precision.HIGHEST,
    )
    with_sin = jnp.dot(
        factors_path,
        factors_mesh[total_vectors:],
        preferred_element_type=jnp.float32,
        precision=lax.Precision.HIGHEST,
    )
    mixing_real = (with_cos[:path_dev] + with_sin[path_dev:]) / k_total
    mixing_imag = (with_cos[path_dev:] - with_sin[:path_dev]) / k_total
    mixing = jnp.concatenate([mixing_real, mixing_imag], 0)
    k_piece = lax.all_gather(arrived, "row", axis=0, tiled=True)
    amount = k_piece.shape[0]
    fourier_amount = k_piece.shape[0]
    factors = phases(lattice, k_order)
    fourier_sum = jnp.dot(
        factors, k_piece.reshape(fourier_amount, -1), preferred_element_type=jnp.float32
    )
    path_sum = jnp.dot(
        mixing,
        k_piece.reshape(amount, -1).astype(jnp.float32),
        preferred_element_type=jnp.float32,
        precision=lax.Precision.HIGHEST,
    )
    summed, path_sum = (fourier_sum, path_sum)
    products = summed.reshape(2, lattice_rows, local_rows, 2, orbitals)
    lattice_f = combine_fourier(products, k_total)
    path_h = combine_path(path_sum.reshape(2, path_dev, local_rows, 2, orbitals))
    lattice_h = lattice_f.astype(jnp.bfloat16)
    return (lattice_h, path_h)


def solution(mesh):
    return jax.shard_map(
        local,
        mesh=mesh,
        in_specs=(
            P(("ka", "row"), None, None, None),
            P(("ka", "row"), None),
            P(),
            P(None, "row"),
            P("row"),
            P(),
        ),
        out_specs=(P("row", "ka", None), P("row", "ka", None)),
        check_vma=False,
    )
```

profile of v0, /device:TPU:0, one launch (start us, length us, event | category | flops | bytes accessed | tf_op | source)
XLA Modules:
  0.0 96.4 jit_solution(5764981165644782622)
XLA Ops:
  7.2 0.0 copy-start
  7.2 0.0 all-gather.3.cloned.1.call-start
  7.2 0.7 reduce
  7.9 1.2 %multiply_convert_fusion = bf16[1,2,384,384]{3,2,1,0:T(8,128)(2,1)S(1)} fusion(bf16[1,2,384,384]{3,2,1,0:T(8,128)(2,1)} %param.6, f32[384]{0:T(512)S(1)} %reduce), kind=kLoop, calls=%fused_computation.23 | loop fusion | flops 884736 | bytes 1181184 | tf_op jit(solution)/shard_map/convert_element_type | solution.py:45
  9.2 1.3 %slice_bitcast_fusion.3 = (bf16[1,384,384]{2,1,0:T(8,128)(2,1)S(1)}, bf16[1,384,384]{2,1,0:T(8,128)(2,1)S(1)}, bf16[1,384,384]{2,1,0:T(8,128)(2,1)S(1)}, bf16[1,384,384]{2,1,0:T(8,128)(2,1)S(1)}) fusion(bf16[1,2,384,384]{3,2,1,0:T(8,128)(2,1)S(1)} %multiply_convert_fusion, bf16[1,2,384,384]{3,2,1,0:T(8,128)(2,1)} %param.6), kind=kLoop, calls=%fused_computation.28 | loop fusion | bytes 2359296 | tf_op jit(solution)/shard_map/squeeze | solution.py:49
  10.5 0.7 fusion.10
  11.1 0.9 copy.83
  12.0 0.5 broadcast.30
  12.6 4.4 %reduce.1 = bf16[384,768]{1,0:T(8,128)(2,1)S(1)} reduce(bf16[384,1,768]{2,1,0:T(2,128)(2,1)S(1)} %bitcast.83, bf16[]{:T(256)} %broadcast.30), dimensions={1}, to_apply=%bitcast.81.reduce_sub_computation | reduce | bytes 1179650
  16.9 0.1 reshape.77
  17.1 23.6 %all_to_all.12 = bf16[8,2,18432]{2,1,0:T(2,128)(2,1)S(1)} all-to-all(bf16[8,2,18432]{2,1,0:T(2,128)(2,1)S(1)} %reshape.77), channel_id=1, replica_groups=mesh['ka'=8,'row'=4] {'ka'}, dimensions={0} | all-to-all | bytes 1179648 | tf_op jit(solution)/shard_map/all_to_all | solution.py:57
  40.7 0.0 copy-start.1
  40.7 0.0 copy-start.2
  40.7 0.0 copy-start.4
  40.7 0.0 copy-start.3
  40.7 0.6 reshape.78
  41.3 0.9 copy.66
  42.2 0.0 all-gather.3.cloned.1.call-update
  42.2 0.0 copy-done.1
  42.2 5.2 %all-gather = s32[4,64,3]{1,2,0:T(4,128)S(1)} all-gather(s32[1,64,3]{1,2,0:T(4,128)S(1)} %bitcast.92), channel_id=1, replica_groups=mesh['ka'=8,'row'=4] {'row'}, dimensions={0}, use_global_device_ids=true | all-gather | bytes 3840 | tf_op jit(solution)/shard_map/all_gather | solution.py:64
  47.4 0.1 reshape.69
  47.5 0.0 copy-done.2
  47.5 0.1 reshape.61
  47.6 0.1 copy.50
  47.7 0.1 mul.87
  47.8 0.1 multiply_reduce_fusion.1
  47.9 0.1 cosine_convert_fusion.1
  47.9 0.1 pad_maximum_fusion.1
  48.0 0.1 convert_element_type.44
  48.1 0.0 copy-done.4
  48.1 0.6 dynamic-slice
  49.4 0.0 copy-done.3
  49.4 0.2 dynamic-update-slice
  49.6 5.2 %all-reduce = s32[256]{0:T(256)S(1)} all-reduce(s32[256]{0:T(256)S(1)} %dynamic-update-slice), channel_id=1, replica_groups=mesh['ka'=8,'row'=4] {'row'}, use_global_device_ids=true, to_apply=%add | all-reduce | flops 256 | bytes 2048
  54.8 0.0 copy-done
  54.8 0.1 constant_dynamic-slice_fusion
  54.9 0.1 multiply_reduce_fusion
  54.9 0.1 multiply_reduce_fusion.2
  55.0 0.1 multiply_convert_fusion.2
  55.1 0.1 multiply_convert_fusion.1
  55.2 0.3 fusion.28
  55.4 0.3 fusion.27
  55.7 9.2 %all-gather.3.cloned.1.call-done = bf16[32,48,768]{2,1,0:T(8,128)(2,1)} async-done(((bf16[8,48,768]{2,1,0:T(8,128)(2,1)}), bf16[32,48,768]{2,1,0:T(8,128)(2,1)}) %all-gather.3.cloned.1.call-update) | async-done | bytes 2359312 | tf_op jit(solution)/shard_map/all_gather | solution.py:86
  64.9 3.8 %copy.71 = bf16[4,8,48,768]{3,1,2,0:T(8,128)(2,1)} copy(bf16[4,8,48,768]{3,2,1,0:T(8,128)(2,1)} %bitcast.86) | data formatting | bytes 4718592
  68.8 3.5 %dot_general.23 = bf16[48,2,384,32]{2,1,0,3:T(2,128)(2,1)S(1)} reshape(bf16[36864,32]{0,1:T(8,128)(2,1)} %bitcast.82) | data formatting | bytes 4718592 | tf_op jit(solution)/shard_map/dot_general | solution.py:90
  72.3 1.5 %fusion.4 = f32[2,2,48,2,384]{4,1,3,2,0:T(2,128)S(1)} fusion(f32[2,2,32,1,1]{2,1,4,3,0:T(2,128)S(1)} %bitcast.91, bf16[48,2,384,32]{2,1,0,3:T(2,128)(2,1)S(1)} %dot_general.23), kind=kOutput, calls=%fused_computation.8 | convolution fusion | flops 56623104 | bytes 2949632 | tf_op jit(solution)/shard_map/dot_general | solution.py:93
  73.8 0.1 fusion.19
  73.9 0.1 fusion.21
  74.0 2.6 %fusion.6 = f32[2,64,48,2,384]{4,1,3,2,0:T(8,128)S(1)} fusion(bf16[48,2,384,32]{2,1,0,3:T(2,128)(2,1)S(1)} %dot_general.23, bf16[2,64,32,1,1]{1,0,2,4,3:T(2,128)(2,1)S(1)} %bitcast.87), kind=kOutput, calls=%fused_computation.10 | convolution fusion | flops 301989888 | bytes 21241856 | tf_op jit(solution)/shard_map/dot_general | solution.py:90
  76.6 0.8 fusion.1
  77.4 0.8 fusion.3
  78.2 0.1 pad_maximum_fusion
  78.3 0.7 copy.61
  79.1 3.3 %fusion = bf16[64,48,768]{2,0,1:T(8,128)(2,1)} fusion(f32[64,48,384]{2,0,1:T(8,128)S(1)} %fusion.1, f32[64,48,384]{2,0,1:T(8,128)S(1)} %fusion.3), kind=kLoop, calls=%fused_computation.1 | loop fusion | flops 7077888 | bytes 14155776 | tf_op jit(solution)/shard_map/convert_element_type | solution.py:103
  82.4 7.1 %copy.60 = bf16[64,48,768]{2,1,0:T(8,128)(2,1)} copy(bf16[64,48,768]{2,0,1:T(8,128)(2,1)} %fusion) | data formatting | bytes 9437184
  (6 shorter events, 0.1 us)
Async XLA Ops:
  7.2 47.6 %copy-start = (s32[3,8]{1,0:T(4,128)S(1)}, s32[3,8]{1,0:T(4,128)}, u32[]{:S(2)}) copy-start(s32[3,8]{1,0:T(4,128)} %param.11) | copy-start | bytes 292
  7.2 57.8 %all-gather.3.cloned.1.call-start = ((), (), s32[]{:S(2)}) async-start(), calls=%async_computation.1 | async-start | bytes 2949120 | tf_op jit(solution)/shard_map/all_gather | solution.py:86
  40.7 1.5 %copy-start.1 = (s32[3,64]{1,0:T(4,128)S(1)}, s32[3,64]{1,0:T(4,128)}, u32[]{:S(2)}) copy-start(s32[3,64]{1,0:T(4,128)} %param.9) | copy-start | bytes 2308
  40.7 6.8 %copy-start.2 = (s32[3,32]{1,0:T(4,128)S(1)}, s32[3,32]{1,0:T(4,128)}, u32[]{:S(2)}) copy-start(s32[3,32]{1,0:T(4,128)} %param.8) | copy-start | bytes 1156
  40.7 7.4 %copy-start.4 = (u32[32]{0:T(128)S(1)}, u32[32]{0:T(128)}, u32[]{:S(2)}) copy-start(u32[32]{0:T(128)} %constant.58) | copy-start | bytes 388
  40.7 8.7 %copy-start.3 = (s32[64]{0:T(128)S(1)}, s32[64]{0:T(128)}, u32[]{:S(2)}) copy-start(s32[64]{0:T(128)} %param.10) | copy-start | bytes 772
Sparse Core Ops, SparseCore 0:
  42.3 22.5 all-gather.2
where the time goes:
time: 96.8 us; the launch traced here: 96.4 us
  blocking collectives  34 us (35%)
  local copies, waits for them, and re-layouts  20.9 us (22%)
  between operations  14.9 us (15%)
  other arithmetic  12 us (12%)
  waiting for transfers between devices  9.25 us (10%)
  matrix products  5.35 us (6%)
    all_to_all x1, blocking collectives, local(): lax.all_to_all(rotated, 'ka', split_axis=1, concat_axis=0, tiled=True)  23.6 us
    unnamed x21, local copies, waits for them, and re-layouts  14.8 us
    all_gather x1, waiting for transfers between devices, local(): k_piece = lax.all_gather(arrived, 'row', axis=0, tiled=True)  9.23 us
    all_gather x1, blocking collectives, local(): lax.all_gather(lattice, 'row', axis=1, tiled=True)  5.19 us
    unnamed x1, blocking collectives  5.15 us
    unnamed x2, other arithmetic  5.07 us
    dot_general x1, local copies, waits for them, and re-layouts, local(): jnp.dot(factors, k_piece.reshape(fourier_amount, -1), preferred_element_t...  3.51 us
    convert_element_type x1, other arithmetic, local(): lattice_h = lattice_f.astype(jnp.bfloat16)  3.29 us
  transfers between devices with their start and end apart: 1, of which 1 were waited for; matrix products, arithmetic and copies ran while one was open for 2% of the time, Pallas kernels for 0%

commit v1 on v0

--- a/solution.py
+++ b/solution.py
@@ -54,7 +54,19 @@
     rotated = jnp.einsum(
         "kna,knb->kab", stacked, partner, preferred_element_type=jnp.float32
     ).astype(jnp.bfloat16)
-    arrived = lax.all_to_all(rotated, "ka", split_axis=1, concat_axis=0, tiled=True)
+
+    def draw_patch(vals, bus_axis, dimension_no, dim_no):
+        return jnp.concatenate(
+            jax.lax.all_to_all(
+                jnp.stack(jnp.split(vals, jax.lax.axis_size(bus_axis), dimension_no), axis=0),
+                axis_name=bus_axis,
+                split_axis=0,
+                concat_axis=0,
+            ),
+            axis=dim_no,
+        )
+
+    arrived = draw_patch(rotated, "ka", dimension_no=1, dim_no=0)
     local_rows = arrived.shape[1]
     lattice_rows = lattice.shape[1]
     k_order = (

time: 96.8 us -> 89.6 us (0.926)
  other arithmetic: 12 us -> 7.64 us
  local copies, waits for them, and re-layouts: 20.9 us -> 17.9 us
    unnamed x2 -> x1, other arithmetic: 5.07 us -> 0.7 us
    unnamed x21 -> x24, local copies, waits for them, and re-layouts: 14.8 us -> 12.7 us
  transfers between devices with their start and end apart: 1 -> 1, of which waited for: 1 -> 1; matrix products, arithmetic and copies ran while one was open for 2% -> 3% of each run, Pallas kernels for 0% -> 0%
where the time goes in v1:
time: 89.6 us; the launch traced here: 89.2 us
  blocking collectives  34.1 us (38%)
  local copies, waits for them, and re-layouts  17.9 us (20%)
  between operations  14.9 us (17%)
  waiting for transfers between devices  9.25 us (10%)
  other arithmetic  7.64 us (9%)
  matrix products  5.37 us (6%)
    all_to_all x1, blocking collectives, draw_patch(): jax.lax.all_to_all(jnp.stack(jnp.split(vals, jax.lax.axis_size(bus_axis),...  23.7 us
    unnamed x24, local copies, waits for them, and re-layouts  12.7 us
    all_gather x1, waiting for transfers between devices, local(): k_piece = lax.all_gather(arrived, 'row', axis=0, tiled=True)  9.23 us
    all_gather x1, blocking collectives, local(): lax.all_gather(lattice, 'row', axis=1, tiled=True)  5.19 us
    unnamed x1, blocking collectives  5.15 us
    dot_general x1, local copies, waits for them, and re-layouts, local(): jnp.dot(factors, k_piece.reshape(fourier_amount, -1), preferred_element_t...  3.51 us
    convert_element_type x1, other arithmetic, local(): lattice_h = lattice_f.astype(jnp.bfloat16)  3.29 us
    dot_general x1, matrix products, local(): jnp.dot(factors, k_piece.reshape(fourier_amount, -1), preferred_element_t...  2.64 us
  transfers between devices with their start and end apart: 1, of which 1 were waited for; matrix products, arithmetic and copies ran while one was open for 3% of the time, Pallas kernels for 0%

profile of v1, /device:TPU:0, one launch (start us, length us, event | category | flops | bytes accessed | tf_op | source)
XLA Modules:
  0.0 89.2 jit_solution(6220958747442360841)
XLA Ops:
  7.2 0.0 copy-start
  7.2 0.0 all-gather.4.cloned.1.call-start
  7.2 0.7 reduce
  7.9 1.2 %multiply_convert_fusion = bf16[1,2,384,384]{3,2,1,0:T(8,128)(2,1)S(1)} fusion(bf16[1,2,384,384]{3,2,1,0:T(8,128)(2,1)} %param.6, f32[384]{0:T(512)S(1)} %reduce), kind=kLoop, calls=%fused_computation.23 | loop fusion | flops 884736 | bytes 1181184 | tf_op jit(solution)/shard_map/convert_element_type | solution.py:45
  9.2 1.3 %slice_bitcast_fusion.3 = (bf16[1,384,384]{2,1,0:T(8,128)(2,1)S(1)}, bf16[1,384,384]{2,1,0:T(8,128)(2,1)S(1)}, bf16[1,384,384]{2,1,0:T(8,128)(2,1)S(1)}, bf16[1,384,384]{2,1,0:T(8,128)(2,1)S(1)}) fusion(bf16[1,2,384,384]{3,2,1,0:T(8,128)(2,1)S(1)} %multiply_convert_fusion, bf16[1,2,384,384]{3,2,1,0:T(8,128)(2,1)} %param.6), kind=kLoop, calls=%fused_computation.28 | loop fusion | bytes 2359296 | tf_op jit(solution)/shard_map/squeeze | solution.py:49
  10.5 0.7 fusion.10
  11.1 0.0 copy-start.1
  11.1 0.0 copy-start.2
  11.2 0.0 copy-start.4
  11.2 0.0 copy-start.3
  11.3 23.7 %all_to_all.5 = bf16[8,1,48,768]{3,2,1,0:T(8,128)(2,1)} all-to-all(bf16[8,1,48,768]{3,2,1,0:T(8,128)(2,1)S(1)} %fusion.22), channel_id=1, replica_groups=mesh['ka'=8,'row'=4] {'ka'}, dimensions={0} | all-to-all | bytes 1179648 | tf_op jit(solution)/shard_map/all_to_all | solution.py:60
  35.0 0.0 all-gather.4.cloned.1.call-update
  35.0 0.0 copy-done.1
  35.0 5.2 %all-gather.1 = s32[4,64,3]{1,2,0:T(4,128)S(1)} all-gather(s32[1,64,3]{1,2,0:T(4,128)S(1)} %bitcast.117), channel_id=1, replica_groups=mesh['ka'=8,'row'=4] {'row'}, dimensions={0}, use_global_device_ids=true | all-gather | bytes 3840 | tf_op jit(solution)/shard_map/all_gather | solution.py:76
  40.2 0.1 reshape.72
  40.3 0.0 copy-done.2
  40.3 0.1 reshape.61
  40.4 0.1 copy.37
  40.5 0.1 mul.87
  40.6 0.1 multiply_reduce_fusion.1
  40.7 0.1 cosine_convert_fusion.1
  40.8 0.1 pad_maximum_fusion.1
  40.9 0.1 convert_element_type.44
  40.9 0.0 copy-done.4
  41.0 0.6 dynamic-slice
  42.2 0.0 copy-done.3
  42.2 0.2 dynamic-update-slice
  42.5 5.2 %all-reduce = s32[256]{0:T(256)S(1)} all-reduce(s32[256]{0:T(256)S(1)} %dynamic-update-slice), channel_id=1, replica_groups=mesh['ka'=8,'row'=4] {'row'}, use_global_device_ids=true, to_apply=%add | all-reduce | flops 256 | bytes 2048
  47.6 0.0 copy-done
  47.6 0.1 constant_dynamic-slice_fusion
  47.7 0.1 multiply_reduce_fusion
  47.8 0.1 multiply_reduce_fusion.2
  47.9 0.1 multiply_convert_fusion.2
  47.9 0.1 multiply_convert_fusion.1
  48.0 0.3 fusion.36
  48.2 0.3 fusion.35
  48.5 9.2 %all-gather.4.cloned.1.call-done = bf16[32,1,48,768]{3,2,1,0:T(8,128)(2,1)} async-done(((bf16[8,1,48,768]{3,2,1,0:T(8,128)(2,1)}), bf16[32,1,48,768]{3,2,1,0:T(8,128)(2,1)}) %all-gather.4.cloned.1.call-update) | async-done | bytes 2359312 | tf_op jit(solution)/shard_map/all_gather | solution.py:98
  57.8 3.8 %copy.56 = bf16[4,8,48,768]{3,1,2,0:T(8,128)(2,1)} copy(bf16[4,8,48,768]{3,2,1,0:T(8,128)(2,1)} %bitcast.111) | data formatting | bytes 4718592
  61.6 3.5 %dot_general.23 = bf16[48,2,384,32]{2,1,0,3:T(2,128)(2,1)S(1)} reshape(bf16[36864,32]{0,1:T(8,128)(2,1)} %bitcast.110) | data formatting | bytes 4718592 | tf_op jit(solution)/shard_map/dot_general | solution.py:102
  65.1 1.5 %fusion.4 = f32[2,2,48,2,384]{4,1,3,2,0:T(2,128)S(1)} fusion(f32[2,2,32,1,1]{2,1,4,3,0:T(2,128)S(1)} %bitcast.116, bf16[48,2,384,32]{2,1,0,3:T(2,128)(2,1)S(1)} %dot_general.23), kind=kOutput, calls=%fused_computation.8 | convolution fusion | flops 56623104 | bytes 2949632 | tf_op jit(solution)/shard_map/dot_general | solution.py:105
  66.7 0.1 fusion.19
  66.7 0.1 fusion.21
  66.8 2.6 %fusion.6 = f32[2,64,48,2,384]{4,1,3,2,0:T(8,128)S(1)} fusion(bf16[48,2,384,32]{2,1,0,3:T(2,128)(2,1)S(1)} %dot_general.23, bf16[2,64,32,1,1]{1,0,2,4,3:T(2,128)(2,1)S(1)} %bitcast.112), kind=kOutput, calls=%fused_computation.10 | convolution fusion | flops 301989888 | bytes 21241856 | tf_op jit(solution)/shard_map/dot_general | solution.py:102
  69.5 0.8 fusion.1
  70.3 0.8 fusion.3
  71.0 0.1 pad_maximum_fusion
  71.2 0.7 copy.47
  71.9 3.3 %fusion = bf16[64,48,768]{2,0,1:T(8,128)(2,1)} fusion(f32[64,48,384]{2,0,1:T(8,128)S(1)} %fusion.1, f32[64,48,384]{2,0,1:T(8,128)S(1)} %fusion.3), kind=kLoop, calls=%fused_computation.1 | loop fusion | flops 7077888 | bytes 14155776 | tf_op jit(solution)/shard_map/convert_element_type | solution.py:115
  75.2 7.1 %copy.46 = bf16[64,48,768]{2,1,0:T(8,128)(2,1)} copy(bf16[64,48,768]{2,0,1:T(8,128)(2,1)} %fusion) | data formatting | bytes 9437184
  (14 shorter events, 0.1 us)
Async XLA Ops:
  7.2 40.5 %copy-start = (s32[3,8]{1,0:T(4,128)S(1)}, s32[3,8]{1,0:T(4,128)}, u32[]{:S(2)}) copy-start(s32[3,8]{1,0:T(4,128)} %param.11) | copy-start | bytes 292
  7.2 50.6 %all-gather.4.cloned.1.call-start = ((), (), s32[]{:S(2)}) async-start(), calls=%async_computation.1 | async-start | bytes 2949120 | tf_op jit(solution)/shard_map/all_gather | solution.py:98
  11.1 23.9 %copy-start.1 = (s32[3,64]{1,0:T(4,128)S(1)}, s32[3,64]{1,0:T(4,128)}, u32[]{:S(2)}) copy-start(s32[3,64]{1,0:T(4,128)} %param.9) | copy-start | bytes 2308
  11.1 29.2 %copy-start.2 = (s32[3,32]{1,0:T(4,128)S(1)}, s32[3,32]{1,0:T(4,128)}, u32[]{:S(2)}) copy-start(s32[3,32]{1,0:T(4,128)} %param.8) | copy-start | bytes 1156
  11.2 29.8 %copy-start.4 = (u32[32]{0:T(128)S(1)}, u32[32]{0:T(128)}, u32[]{:S(2)}) copy-start(u32[32]{0:T(128)} %constant.58) | copy-start | bytes 388
  11.2 31.0 %copy-start.3 = (s32[64]{0:T(128)S(1)}, s32[64]{0:T(128)}, u32[]{:S(2)}) copy-start(s32[64]{0:T(128)} %param.10) | copy-start | bytes 772
Sparse Core Ops, SparseCore 0:
  35.2 22.5 all-gather.3
